TPU v7x, 128 devices: a whole 4x4x4 slice. The times are simulated.
128 devices in a mesh: dp: 4 (over x), cp: 32 (over z, y, core).
Axes of the slice: x: 4, y: 4, z: 4, core: 2. Of those that a mesh axis runs over, the one named last changes fastest.
Arguments:
- tokens: bfloat16 [4, 4096, 4096], P('dp', 'cp'), may hold values from -60 to 60
- qkv_weight: bfloat16 [4096, 3072], replicated, may hold values from -0.09375 to 0.09375
- owner_slot: int32 [4, 32], P('dp', 'cp'), may hold values from 0 to 3, as said below
- slab_sequence: int32 [4, 32], replicated, may hold values from 0 to 16, as said below
- slab_order: int32 [4, 32], replicated, may hold values from 0 to 15, as said below
Outputs:
- context: bfloat16 [4, 4096, 2048], P('dp', 'cp')
Inputs may be any that keep to these rules, and one draw needn't show every extreme that they name: For every column c, the entries owner_slot[a, c] over all rows a are 0 to 3, each once. `slab_sequence`: in each row, the slabs with one sequence number carry the orders 0 to L-1, each once, L being their count; no sequence has more than 16 slabs. `slab_order`: see slab_sequence.
All inputs are finite; a program needn't handle non-finite values.
Results may differ from a plain program's by a relative error of at most 0.006.
The roundings to bfloat16 on the way count: a program that leaves them out, or rounds other values in their place, can miss the bound.
Values may be sent and summed in bfloat16 or wider, within the bound.
No kernel may reach another device: no remote copies, remote signals or barrier semaphores. Data moves between devices by JAX's collectives and lax.ppermute only.
A program may use at most 128 MiB of HBM per device.

v0:
```python
import jax
import jax.numpy as jnp
from jax import lax
from jax.sharding import PartitionSpec as P

QH = 16
KVH = 4
HD = 128
ROPE_BASE = 500000.0
NEG_FILL = -1e30


def rotate(heads, positions):
    half_dim = heads.shape[-1] // 2
    frequency = ROPE_BASE ** (-jnp.arange(half_dim, dtype=jnp.float32) * 2.0 / heads.shape[-1])
    angles = positions.astype(jnp.float32)[:, None] * frequency[None, :]
    cosine = jnp.cos(angles)[:, None, :]
    sine_part = jnp.sin(angles)[:, None, :]
    first_half = heads[..., :half_dim]
    second_half = heads[..., half_dim:]
    return jnp.concatenate(
        [
            first_half * cosine - second_half * sine_part,
            second_half * cosine + first_half * sine_part,
        ],
        axis=-1,
    )


def project(input_rows, weight, positions):
    projected = jnp.dot(input_rows, weight, preferred_element_type=jnp.float32)
    count_rows = input_rows.shape[0]
    query = rotate(projected[:, : QH * HD].reshape(count_rows, QH, HD), positions).astype(
        jnp.bfloat16
    )
    key_heads = rotate(
        projected[:, QH * HD : (QH + KVH) * HD].reshape(count_rows, KVH, HD), positions
    ).astype(jnp.bfloat16)
    value_heads = projected[:, (QH + KVH) * HD :].astype(jnp.bfloat16)
    key_value = jnp.concatenate([key_heads.reshape(count_rows, KVH * HD), value_heads], axis=1)
    return (query.reshape(count_rows, QH * HD), key_value)


def local(tokens, qkv_weight, owner_slot, slab_sequence, slab_order):
    loader_rows = tokens[0]
    local_targets = owner_slot[0]
    slab_count = local_targets.shape[0]
    tok_dev = loader_rows.shape[0]
    slab_len = tok_dev // slab_count
    groups_count = lax.axis_size("dp")
    my_row = lax.axis_index("dp")
    column = lax.axis_index("cp")
    row_slabs = slab_sequence.shape[1]
    row_tok = row_slabs * slab_len
    group_size = QH // KVH
    offsets = jnp.arange(slab_len, dtype=jnp.int32)
    destinations = jnp.arange(groups_count * slab_count, dtype=jnp.int32)
    selector = (local_targets[None, :] == destinations[:, None]).astype(jnp.bfloat16)
    own_order = lax.dynamic_slice(slab_order, (my_row, column * slab_count), (1, slab_count))[0]
    own_pos = (own_order[:, None] * slab_len + offsets[None, :]).reshape(tok_dev)
    sent_row = local_targets // slab_count
    sent_slab = column * slab_count + local_targets % slab_count
    sent_order = slab_order[sent_row, sent_slab]
    sent_pos = (sent_order[:, None] * slab_len + offsets[None, :]).reshape(tok_dev)
    query_local, key_value_local = project(loader_rows, qkv_weight, sent_pos)
    combined = jnp.concatenate([query_local, key_value_local], axis=1)
    col_width = combined.shape[1]
    packed = jnp.einsum(
        "pj,jtd->ptd",
        selector,
        combined.reshape(slab_count, slab_len, col_width),
        preferred_element_type=jnp.float32,
    )
    received = lax.all_to_all(
        packed.astype(jnp.bfloat16).reshape(groups_count * slab_count * slab_len, col_width),
        "dp",
        split_axis=0,
        concat_axis=0,
        tiled=True,
    )
    unpack_col_width = received.shape[1]
    received = jnp.sum(
        received.reshape(groups_count, tok_dev, unpack_col_width), axis=0, dtype=jnp.float32
    ).astype(jnp.bfloat16)
    query = received[:, : QH * HD]
    key_value = received[:, QH * HD :]
    row_sequence = lax.dynamic_index_in_dim(slab_sequence, my_row, 0, keepdims=False)
    row_order = lax.dynamic_index_in_dim(slab_order, my_row, 0, keepdims=False)
    code_row = (
        row_sequence[:, None] * row_tok + row_order[:, None] * slab_len + offsets[None, :]
    ).reshape(row_tok)
    query_code = lax.dynamic_slice_in_dim(code_row, column * tok_dev, tok_dev)
    seq_start = query_code - own_pos
    query_groups = query.reshape(tok_dev, KVH, group_size, HD)
    score_scale = HD ** (-0.5)

    def update(state_now, block_keys, key_code):
        row_peak, denom_sum, weighted = state_now
        block_rows = block_keys.shape[0]
        allowed = (key_code[None, :] <= query_code[:, None]) & (
            key_code[None, :] >= seq_start[:, None]
        )

        def compute(state_in):
            peak_in, denom_in, weighted_in = state_in
            key_part = block_keys[:, : KVH * HD].reshape(block_rows, KVH, HD)
            value_part = block_keys[:, KVH * HD :].reshape(block_rows, KVH, HD)
            scores = (
                jnp.einsum(
                    "tgjh,ngh->gjtn", query_groups, key_part, preferred_element_type=jnp.float32
                )
                * score_scale
            )
            scores = jnp.where(allowed, scores, NEG_FILL)
            new_peak = jnp.maximum(peak_in, jnp.max(scores, axis=-1))
            weights = jnp.where(allowed, jnp.exp(scores - new_peak[..., None]), 0.0)
            rescale = jnp.exp(peak_in - new_peak)
            denom_out = denom_in * rescale + jnp.sum(weights, axis=-1)
            product = jnp.einsum(
                "gjtn,ngh->gjth",
                weights.astype(jnp.bfloat16),
                value_part,
                preferred_element_type=jnp.float32,
            )
            return (new_peak, denom_out, weighted_in * rescale[..., None] + product)

        return lax.cond(
            jnp.any(allowed), compute, lambda state_in: state_in, (row_peak, denom_sum, weighted)
        )

    start_state = (
        jnp.full((KVH, group_size, tok_dev), NEG_FILL, jnp.float32),
        jnp.zeros((KVH, group_size, tok_dev), jnp.float32),
        jnp.zeros((KVH, group_size, tok_dev, HD), jnp.float32),
    )
    shard_rows = lax.all_gather(key_value, "cp", axis=0, tiled=True)
    count_keys = shard_rows.shape[0]
    key_code = code_row
    step_rows = 1024
    steps_count = count_keys // step_rows

    def scan_step(state_in, pieces):
        return (update(state_in, pieces[0], pieces[1]), None)

    state_out, unused = lax.scan(
        scan_step,
        start_state,
        (
            shard_rows.reshape(steps_count, step_rows, shard_rows.shape[1]),
            key_code.reshape(steps_count, step_rows),
        ),
    )
    row_peak, denom_sum, weighted = state_out
    context = (weighted / denom_sum[..., None]).transpose(2, 0, 1, 3).reshape(tok_dev, QH * HD)
    return context.astype(jnp.bfloat16)[None]


def solution(mesh):
    in_specs = (P("dp", "cp", None), P(), P("dp", "cp"), P(), P())
    out_specs = P("dp", "cp", None)
    return jax.shard_map(local, mesh=mesh, in_specs=in_specs, out_specs=out_specs, check_vma=False)
```

profile of v0, /device:TPU:9, one launch (start us, length us, event | category | flops | bytes accessed | tf_op | source)
XLA Modules:
  0.0 182.6 jit_solution(14069714040307647107)
XLA Ops:
  7.8 10.0 %fusion.13 = f32[128,3072]{1,0:T(8,128)S(1)} fusion(bf16[4096,3072]{1,0:T(8,128)(2,1)} %param.10, bf16[1,128,4096]{2,1,0:T(8,128)(2,1)S(1)} %copy-done), kind=kOutput, calls=%fused_computation.19 | convolution fusion | flops 3221225472 | bytes 27787264 | tf_op jit(solution)/shard_map/dot_general | solution.py:31
  22.6 40.6 %all_to_all.6 = bf16[4,128,3072]{2,1,0:T(8,128)(2,1)} all-to-all(bf16[4,128,3072]{2,1,0:T(8,128)(2,1)S(1)} %multiply_convert_fusion), channel_id=1, replica_groups=mesh['dp'=4,'cp'=32] {'dp'}, dimensions={0} | all-to-all | bytes 6291456 | tf_op jit(solution)/shard_map/all_to_all | solution.py:74
  63.2 2.5 %reduce_sum.22 = bf16[128,3072]{1,0:T(8,128)(2,1)S(1)} reduce(bf16[4,128,3072]{2,1,0:T(8,128)(2,1)} %all_to_all.6, bf16[]{:T(256)} %constant.95.clone.1), dimensions={0}, to_apply=%region_0.1 | reduce | flops 1179648 | bytes 3932162 | tf_op jit(solution)/shard_map/reduce_sum | solution.py:82
  70.0 51.5 %all-gather.2.cloned.1.call-done = bf16[4096,1024]{1,0:T(8,128)(2,1)} async-done(((bf16[128,1024]{1,0:T(8,128)(2,1)}), bf16[4096,1024]{1,0:T(8,128)(2,1)}) %all-gather.2.cloned.1.call-update) | async-done | bytes 8388624 | tf_op jit(solution)/shard_map/all_gather | solution.py:136
  121.5 11.4 %copy.18 = bf16[4,1024,1024]{1,2,0:T(8,128)(2,1)} copy(bf16[4,1024,1024]{2,1,0:T(8,128)(2,1)} %bitcast.79) | data formatting | bytes 16777216 | tf_op jit(solution)/shard_map/while | solution.py:145
  133.0 40.7 %while.15 = (s32[]{:T(128)}, f32[4,4,128]{2,1,0:T(4,128)S(1)}, f32[4,4,128]{2,1,0:T(4,128)S(1)}, f32[4,4,128,128]{3,2,1,0:T(8,128)S(1)}, s32[4,1024]{1,0:T(4,128...) while((s32[]{:T(128)}, f32[4,4,128]{2,1,0:T(4,128)S(1)}, ...), condition=%wide.region_7.8_spmd, body=%wide.region_1.7_spmd.sunk | while | flops 1102057472 | bytes 38941920 | solution.py:145
  134.6 8.6 %conditional.2 = ((f32[4,4,128]{2,1,0:T(4,128)S(1)}, f32[4,4,128]{2,1,0:T(4,128)S(1)}, f32[4,4,128,128]{3,2,1,0:T(8,128)S(1)})) conditional(s32[]{:T(128)} %convert_element_type.65, (f32[4,4,128]{2,1,0:T(4,128)S(1)}, f32[4,4,128]{2,1,0:T(4,128)S(1)}, f32[4,4,128,128]{3,2,1,0:T(8,128)S(1)}) %tuple.49, (pred[128,1024]{0,1:T(8,128)(4,1)S(1)}, ...), branch_computations={%region_3.3_spmd, %region_4.6_spmd} | conditional | flops 1101533184 | bytes 38797348 | solution.py:127
  134.6 1.8 dynamic-slice_bitcast_fusion
  138.0 2.0 %fusion.2 = f32[4,4,128]{2,1,0:T(4,128)S(1)} fusion(f32[4,1024,128,4]{2,1,3,0:T(8,128)S(1)} %get-tuple-element.158, f32[4,4,128]{2,1,0:T(4,128)S(1)} %max.3, pred[128,1024]{0,1:T(8,128)(4,1)S(1)} %get-tuple-element.79), kind=kLoop, calls=%fused_computation.4 | loop fusion | flops 10483712 | bytes 8536064 | tf_op jit(solution)/shard_map/while/body/eval_jaxpr/cond/branch_1_fun/reduce_sum | solution.py:118
  140.1 3.1 %fusion.6 = f32[4,4,128,128]{3,2,1,0:T(8,128)S(1)} fusion(bf16[1024,4,128,1]{0,2,3,1:T(8,128)(2,1)S(1)} %bitcast.77, f32[4,1024,128,4]{2,1,3,0:T(8,128)S(1)} %get-tuple-element.158, f32[4,4,128]{2,1,0:T(4,128)S(1)} %max.3, pred[128,1024]{0,1:T(8,128)(4,1)S(1)} %get-tuple-element.79, f32[4,4,128,128]{3,2,1,0:T(8,128)S(1)} %get-tuple-element.84, ...), kind=kOutput, calls=%fused_computation.8 | convolution fusion | flops 547880960 | bytes 11681792 | tf_op jit(solution)/shard_map/while/body/eval_jaxpr/cond/branch_1_fun/gjtn,ngh->gjth/dot_general | solution.py:119
  144.7 8.6 %conditional.2 = ((f32[4,4,128]{2,1,0:T(4,128)S(1)}, f32[4,4,128]{2,1,0:T(4,128)S(1)}, f32[4,4,128,128]{3,2,1,0:T(8,128)S(1)})) conditional(s32[]{:T(128)} %convert_element_type.65, (f32[4,4,128]{2,1,0:T(4,128)S(1)}, f32[4,4,128]{2,1,0:T(4,128)S(1)}, f32[4,4,128,128]{3,2,1,0:T(8,128)S(1)}) %tuple.49, (pred[128,1024]{0,1:T(8,128)(4,1)S(1)}, ...), branch_computations={%region_3.3_spmd, %region_4.6_spmd} | conditional | flops 1101533184 | bytes 38797348 | solution.py:127
  144.7 1.8 dynamic-slice_bitcast_fusion
  146.7 1.5 fusion
  148.2 2.0 %fusion.2 = f32[4,4,128]{2,1,0:T(4,128)S(1)} fusion(f32[4,1024,128,4]{2,1,3,0:T(8,128)S(1)} %get-tuple-element.158, f32[4,4,128]{2,1,0:T(4,128)S(1)} %max.3, pred[128,1024]{0,1:T(8,128)(4,1)S(1)} %get-tuple-element.79), kind=kLoop, calls=%fused_computation.4 | loop fusion | flops 10483712 | bytes 8536064 | tf_op jit(solution)/shard_map/while/body/eval_jaxpr/cond/branch_1_fun/reduce_sum | solution.py:118
  150.2 3.1 %fusion.6 = f32[4,4,128,128]{3,2,1,0:T(8,128)S(1)} fusion(bf16[1024,4,128,1]{0,2,3,1:T(8,128)(2,1)S(1)} %bitcast.77, f32[4,1024,128,4]{2,1,3,0:T(8,128)S(1)} %get-tuple-element.158, f32[4,4,128]{2,1,0:T(4,128)S(1)} %max.3, pred[128,1024]{0,1:T(8,128)(4,1)S(1)} %get-tuple-element.79, f32[4,4,128,128]{3,2,1,0:T(8,128)S(1)} %get-tuple-element.84, ...), kind=kOutput, calls=%fused_computation.8 | convolution fusion | flops 547880960 | bytes 11681792 | tf_op jit(solution)/shard_map/while/body/eval_jaxpr/cond/branch_1_fun/gjtn,ngh->gjth/dot_general | solution.py:119
  154.9 8.6 %conditional.2 = ((f32[4,4,128]{2,1,0:T(4,128)S(1)}, f32[4,4,128]{2,1,0:T(4,128)S(1)}, f32[4,4,128,128]{3,2,1,0:T(8,128)S(1)})) conditional(s32[]{:T(128)} %convert_element_type.65, (f32[4,4,128]{2,1,0:T(4,128)S(1)}, f32[4,4,128]{2,1,0:T(4,128)S(1)}, f32[4,4,128,128]{3,2,1,0:T(8,128)S(1)}) %tuple.49, (pred[128,1024]{0,1:T(8,128)(4,1)S(1)}, ...), branch_computations={%region_3.3_spmd, %region_4.6_spmd} | conditional | flops 1101533184 | bytes 38797348 | solution.py:127
  154.9 1.8 dynamic-slice_bitcast_fusion
  158.4 2.0 %fusion.2 = f32[4,4,128]{2,1,0:T(4,128)S(1)} fusion(f32[4,1024,128,4]{2,1,3,0:T(8,128)S(1)} %get-tuple-element.158, f32[4,4,128]{2,1,0:T(4,128)S(1)} %max.3, pred[128,1024]{0,1:T(8,128)(4,1)S(1)} %get-tuple-element.79), kind=kLoop, calls=%fused_computation.4 | loop fusion | flops 10483712 | bytes 8536064 | tf_op jit(solution)/shard_map/while/body/eval_jaxpr/cond/branch_1_fun/reduce_sum | solution.py:118
  160.4 3.1 %fusion.6 = f32[4,4,128,128]{3,2,1,0:T(8,128)S(1)} fusion(bf16[1024,4,128,1]{0,2,3,1:T(8,128)(2,1)S(1)} %bitcast.77, f32[4,1024,128,4]{2,1,3,0:T(8,128)S(1)} %get-tuple-element.158, f32[4,4,128]{2,1,0:T(4,128)S(1)} %max.3, pred[128,1024]{0,1:T(8,128)(4,1)S(1)} %get-tuple-element.79, f32[4,4,128,128]{3,2,1,0:T(8,128)S(1)} %get-tuple-element.84, ...), kind=kOutput, calls=%fused_computation.8 | convolution fusion | flops 547880960 | bytes 11681792 | tf_op jit(solution)/shard_map/while/body/eval_jaxpr/cond/branch_1_fun/gjtn,ngh->gjth/dot_general | solution.py:119
  165.1 8.6 %conditional.2 = ((f32[4,4,128]{2,1,0:T(4,128)S(1)}, f32[4,4,128]{2,1,0:T(4,128)S(1)}, f32[4,4,128,128]{3,2,1,0:T(8,128)S(1)})) conditional(s32[]{:T(128)} %convert_element_type.65, (f32[4,4,128]{2,1,0:T(4,128)S(1)}, f32[4,4,128]{2,1,0:T(4,128)S(1)}, f32[4,4,128,128]{3,2,1,0:T(8,128)S(1)}) %tuple.49, (pred[128,1024]{0,1:T(8,128)(4,1)S(1)}, ...), branch_computations={%region_3.3_spmd, %region_4.6_spmd} | conditional | flops 1101533184 | bytes 38797348 | solution.py:127
  165.1 1.8 dynamic-slice_bitcast_fusion
  167.1 1.5 fusion
  168.6 2.0 %fusion.2 = f32[4,4,128]{2,1,0:T(4,128)S(1)} fusion(f32[4,1024,128,4]{2,1,3,0:T(8,128)S(1)} %get-tuple-element.158, f32[4,4,128]{2,1,0:T(4,128)S(1)} %max.3, pred[128,1024]{0,1:T(8,128)(4,1)S(1)} %get-tuple-element.79), kind=kLoop, calls=%fused_computation.4 | loop fusion | flops 10483712 | bytes 8536064 | tf_op jit(solution)/shard_map/while/body/eval_jaxpr/cond/branch_1_fun/reduce_sum | solution.py:118
  170.6 3.1 %fusion.6 = f32[4,4,128,128]{3,2,1,0:T(8,128)S(1)} fusion(bf16[1024,4,128,1]{0,2,3,1:T(8,128)(2,1)S(1)} %bitcast.77, f32[4,1024,128,4]{2,1,3,0:T(8,128)S(1)} %get-tuple-element.158, f32[4,4,128]{2,1,0:T(4,128)S(1)} %max.3, pred[128,1024]{0,1:T(8,128)(4,1)S(1)} %get-tuple-element.79, f32[4,4,128,128]{3,2,1,0:T(8,128)S(1)} %get-tuple-element.84, ...), kind=kOutput, calls=%fused_computation.8 | convolution fusion | flops 547880960 | bytes 11681792 | tf_op jit(solution)/shard_map/while/body/eval_jaxpr/cond/branch_1_fun/gjtn,ngh->gjth/dot_general | solution.py:119
  (70 shorter events, 17.5 us)
Async XLA Ops:
  6.5 1.2 copy-start
  6.5 115.0 %all-gather.2.cloned.1.call-start = ((), (), s32[]{:S(2)}) async-start(), calls=%async_computation.1 | async-start | bytes 8650752 | tf_op jit(solution)/shard_map/all_gather | solution.py:136
  7.8 10.8 %copy-start.2 = (s32[4,32]{1,0:T(4,128)S(1)}, s32[4,32]{1,0:T(4,128)}, u32[]{:S(2)}) copy-start(s32[4,32]{1,0:T(4,128)} %param.13) | copy-start | bytes 1540
  173.7 2.0 %copy-start.1 = (bf16[1,128,4096]{2,1,0:T(8,128)(2,1)S(1)}, bf16[1,128,4096]{2,1,0:T(8,128)(2,1)}, u32[]{:S(2)}) copy-start(bf16[1,128,4096]{2,1,0:T(8,128)(2,1)} %param.9) | copy-start | bytes 3145732
Sparse Core Ops, SparseCore 0:
  66.6 54.8 all-gather.1
where the time goes:
time: 183 us
  waiting for transfers between devices  51.6 us (28%)
  blocking collectives  40.6 us (22%)
  matrix products  28.4 us (16%)
  local copies, waits for them, and re-layouts  25.3 us (14%)
  other arithmetic  18.2 us (10%)
  between operations  15.4 us (8%)
  loops' own time  2.98 us (2%)
    all_gather x1, waiting for transfers between devices, local(): shard_rows = lax.all_gather(key_value, 'cp', axis=0, tiled=True)  51.5 us
    all_to_all x1, blocking collectives, local(): lax.all_to_all(packed.astype(jnp.bfloat16).reshape(groups_count * slab_co...  40.6 us
    dot_general x4, matrix products, compute(): jnp.einsum('gjtn,ngh->gjth', weights.astype(jnp.bfloat16), value_part, pr...  12.4 us
    while x2, local copies, waits for them, and re-layouts, local(): lax.scan(scan_step, start_state, (shard_rows.reshape(steps_count, step_ro...  11.7 us
    dot_general x1, matrix products, project(): projected = jnp.dot(input_rows, weight, preferred_element_type=jnp.float32)  9.99 us
    reduce_sum x4, other arithmetic, compute(): denom_out = denom_in * rescale + jnp.sum(weights, axis=-1)  8.07 us
    squeeze x4, local copies, waits for them, and re-layouts, local(): lax.scan(scan_step, start_state, (shard_rows.reshape(steps_count, step_ro...  7.07 us
    dot_general x4, matrix products, compute(): jnp.einsum('tgjh,ngh->gjtn', query_groups, key_part, preferred_element_ty...  5.98 us
  transfers between devices with their start and end apart: 1, of which 1 were waited for; matrix products, arithmetic and copies ran while one was open for 2% of the time, Pallas kernels for 0%

commit v1 on v0

--- a/solution.py
+++ b/solution.py
@@ -133,7 +133,10 @@
         jnp.zeros((KVH, group_size, tok_dev), jnp.float32),
         jnp.zeros((KVH, group_size, tok_dev, HD), jnp.float32),
     )
-    shard_rows = lax.all_gather(key_value, "cp", axis=0, tiled=True)
+    t_next = lax.psum(1, "cp")
+    y = jnp.stack([key_value] * t_next, axis=0)
+    long_array = lax.all_to_all(y, "cp", 0, 0)
+    shard_rows = jnp.concatenate(long_array, axis=0)
     count_keys = shard_rows.shape[0]
     key_code = code_row
     step_rows = 1024

time: 183 us -> 230 us (1.26); the launches traced: 183 us -> 227 us
  waiting for transfers between devices: 51.6 us -> 95.4 us
  between operations: 15.4 us -> 2.15 us
  starting transfers between devices: 0.01 us -> 10 us
  local copies, waits for them, and re-layouts: 25.3 us -> 29 us
    all_to_all x0 -> x1, waiting for transfers between devices: none -> 95.4 us  [local(): long_array = lax.all_to_all(y, 'cp', 0, 0)]
    all_gather x1 -> x0, waiting for transfers between devices: 51.5 us -> none  [local(): shard_rows = lax.all_gather(key_value, 'cp', axis=0, tiled=True)]
    all_to_all x0 -> x1, starting transfers between devices: none -> 10 us  [local(): long_array = lax.all_to_all(y, 'cp', 0, 0)]
    another operation x0 -> x1, local copies, waits for them, and re-layouts: none -> 4.29 us  [local(): y = jnp.stack([key_value] * t_next, axis=0)]
  transfers between devices with their start and end apart: 1 -> 1, of which waited for: 1 -> 1; matrix products, arithmetic and copies ran while one was open for 2% -> 1% of each run, Pallas kernels for 0% -> 0%
where the time goes in v1:
time: 230 us; the launch traced here: 227 us
  waiting for transfers between devices  95.4 us (41%)
  blocking collectives  40.6 us (18%)
  local copies, waits for them, and re-layouts  29 us (13%)
  matrix products  28.4 us (12%)
  other arithmetic  18.2 us (8%)
  starting transfers between devices  10 us (4%)
  loops' own time  2.86 us (1%)
    all_to_all x1, waiting for transfers between devices, local(): long_array = lax.all_to_all(y, 'cp', 0, 0)  95.4 us
    all_to_all x1, blocking collectives, local(): lax.all_to_all(packed.astype(jnp.bfloat16).reshape(groups_count * slab_co...  40.6 us
    dot_general x4, matrix products, compute(): jnp.einsum('gjtn,ngh->gjth', weights.astype(jnp.bfloat16), value_part, pr...  12.4 us
    while x2, local copies, waits for them, and re-layouts, local(): lax.scan(scan_step, start_state, (shard_rows.reshape(steps_count, step_ro...  11.7 us
    all_to_all x1, starting transfers between devices, local(): long_array = lax.all_to_all(y, 'cp', 0, 0)  10 us
    dot_general x1, matrix products, project(): projected = jnp.dot(input_rows, weight, preferred_element_type=jnp.float32)  9.99 us
    reduce_sum x4, other arithmetic, compute(): denom_out = denom_in * rescale + jnp.sum(weights, axis=-1)  8.07 us
    squeeze x4, local copies, waits for them, and re-layouts, local(): lax.scan(scan_step, start_state, (shard_rows.reshape(steps_count, step_ro...  7.07 us
  transfers between devices with their start and end apart: 1, of which 1 were waited for; matrix products, arithmetic and copies ran while one was open for 1% of the time, Pallas kernels for 0%

profile of v1, /device:TPU:9, one launch (start us, length us, event | category | flops | bytes accessed | tf_op | source)
XLA Modules:
  0.0 226.6 jit_solution(10662313251106367042)
XLA Ops:
  1.2 10.0 %fusion.13 = f32[128,3072]{1,0:T(8,128)S(1)} fusion(bf16[4096,3072]{1,0:T(8,128)(2,1)} %param.10, bf16[1,128,4096]{2,1,0:T(8,128)(2,1)S(1)} %copy-done), kind=kOutput, calls=%fused_computation.19 | convolution fusion | flops 3221225472 | bytes 27787264 | tf_op jit(solution)/shard_map/dot_general | solution.py:31
  16.1 40.6 %all_to_all.11 = bf16[4,128,3072]{2,1,0:T(8,128)(2,1)} all-to-all(bf16[4,128,3072]{2,1,0:T(8,128)(2,1)S(1)} %multiply_convert_fusion), channel_id=1, replica_groups=mesh['dp'=4,'cp'=32] {'dp'}, dimensions={0} | all-to-all | bytes 6291456 | tf_op jit(solution)/shard_map/all_to_all | solution.py:74
  56.8 2.5 %reduce_sum.22 = bf16[128,3072]{1,0:T(8,128)(2,1)S(1)} reduce(bf16[4,128,3072]{2,1,0:T(8,128)(2,1)} %all_to_all.11, bf16[]{:T(256)} %constant.95.clone.1), dimensions={0}, to_apply=%region_0.1 | reduce | flops 1179648 | bytes 3932162 | tf_op jit(solution)/shard_map/reduce_sum | solution.py:82
  59.3 4.3 %stack.2 = bf16[32,128,1024]{2,1,0:T(8,128)(2,1)} broadcast(bf16[128,1024]{1,0:T(8,128)(2,1)S(1)} %slice.65), dimensions={1,2} | broadcast | bytes 8650752 | tf_op jit(solution)/shard_map/stack | solution.py:137
  63.6 10.0 %all-to-all-start.1 = ((bf16[32,128,1024]{2,1,0:T(8,128)(2,1)}), bf16[32,128,1024]{2,1,0:T(8,128)(2,1)}, u32[]{:S(2)}, u32[]{:S(2)}) async-start(bf16[32,128,1024]{2,1,0:T(8,128)(2,1)} %stack.2), calls=%async_computation.1 | async-start | bytes 16777216 | tf_op jit(solution)/shard_map/all_to_all | solution.py:138
  77.1 95.4 %all-to-all-done.1 = bf16[32,128,1024]{2,1,0:T(8,128)(2,1)} async-done(((bf16[32,128,1024]{2,1,0:T(8,128)(2,1)}), bf16[32,128,1024]{2,1,0:T(8,128)(2,1)}, u32[]{:S(2)}, u32[]{:S(2)}) %all-to-all-start.1) | async-done | bytes 8388640 | tf_op jit(solution)/shard_map/all_to_all | solution.py:138
  172.5 11.4 %copy.25 = bf16[4,1024,1024]{1,2,0:T(8,128)(2,1)} copy(bf16[4,1024,1024]{2,1,0:T(8,128)(2,1)} %bitcast.18) | data formatting | bytes 16777216 | tf_op jit(solution)/shard_map/while | solution.py:148
  184.0 40.6 %while.15 = (s32[]{:T(128)}, f32[4,4,128]{2,1,0:T(4,128)S(1)}, f32[4,4,128]{2,1,0:T(4,128)S(1)}, f32[4,4,128,128]{3,2,1,0:T(8,128)S(1)}, s32[4,1024]{1,0:T(4,128...) while((s32[]{:T(128)}, f32[4,4,128]{2,1,0:T(4,128)S(1)}, ...), condition=%wide.region_7.8_spmd, body=%wide.region_1.7_spmd.sunk | while | flops 1102057472 | bytes 38941920 | solution.py:148
  185.5 8.6 %conditional.2 = ((f32[4,4,128]{2,1,0:T(4,128)S(1)}, f32[4,4,128]{2,1,0:T(4,128)S(1)}, f32[4,4,128,128]{3,2,1,0:T(8,128)S(1)})) conditional(s32[]{:T(128)} %convert_element_type.65, (f32[4,4,128]{2,1,0:T(4,128)S(1)}, f32[4,4,128]{2,1,0:T(4,128)S(1)}, f32[4,4,128,128]{3,2,1,0:T(8,128)S(1)}) %tuple.50, (pred[128,1024]{0,1:T(8,128)(4,1)S(1)}, ...), branch_computations={%region_3.3_spmd, %region_4.6_spmd} | conditional | flops 1101533184 | bytes 38797348 | solution.py:127
  185.6 1.8 dynamic-slice_bitcast_fusion
  189.0 2.0 fusion.2
  191.1 3.1 %fusion.6 = f32[4,4,128,128]{3,2,1,0:T(8,128)S(1)} fusion(bf16[1024,4,128,1]{0,2,3,1:T(8,128)(2,1)S(1)} %bitcast.77, f32[4,1024,128,4]{2,1,3,0:T(8,128)S(1)} %get-tuple-element.167, f32[4,4,128]{2,1,0:T(4,128)S(1)} %max.3, pred[128,1024]{0,1:T(8,128)(4,1)S(1)} %get-tuple-element.79, f32[4,4,128,128]{3,2,1,0:T(8,128)S(1)} %get-tuple-element.84, ...), kind=kOutput, calls=%fused_computation.8 | convolution fusion | flops 547880960 | bytes 11681792 | tf_op jit(solution)/shard_map/while/body/eval_jaxpr/cond/branch_1_fun/gjtn,ngh->gjth/dot_general | solution.py:119
  195.7 8.6 %conditional.2 = ((f32[4,4,128]{2,1,0:T(4,128)S(1)}, f32[4,4,128]{2,1,0:T(4,128)S(1)}, f32[4,4,128,128]{3,2,1,0:T(8,128)S(1)})) conditional(s32[]{:T(128)} %convert_element_type.65, (f32[4,4,128]{2,1,0:T(4,128)S(1)}, f32[4,4,128]{2,1,0:T(4,128)S(1)}, f32[4,4,128,128]{3,2,1,0:T(8,128)S(1)}) %tuple.50, (pred[128,1024]{0,1:T(8,128)(4,1)S(1)}, ...), branch_computations={%region_3.3_spmd, %region_4.6_spmd} | conditional | flops 1101533184 | bytes 38797348 | solution.py:127
  195.7 1.8 dynamic-slice_bitcast_fusion
  199.2 2.0 fusion.2
  201.2 3.1 %fusion.6 = f32[4,4,128,128]{3,2,1,0:T(8,128)S(1)} fusion(bf16[1024,4,128,1]{0,2,3,1:T(8,128)(2,1)S(1)} %bitcast.77, f32[4,1024,128,4]{2,1,3,0:T(8,128)S(1)} %get-tuple-element.167, f32[4,4,128]{2,1,0:T(4,128)S(1)} %max.3, pred[128,1024]{0,1:T(8,128)(4,1)S(1)} %get-tuple-element.79, f32[4,4,128,128]{3,2,1,0:T(8,128)S(1)} %get-tuple-element.84, ...), kind=kOutput, calls=%fused_computation.8 | convolution fusion | flops 547880960 | bytes 11681792 | tf_op jit(solution)/shard_map/while/body/eval_jaxpr/cond/branch_1_fun/gjtn,ngh->gjth/dot_general | solution.py:119
  205.8 8.6 %conditional.2 = ((f32[4,4,128]{2,1,0:T(4,128)S(1)}, f32[4,4,128]{2,1,0:T(4,128)S(1)}, f32[4,4,128,128]{3,2,1,0:T(8,128)S(1)})) conditional(s32[]{:T(128)} %convert_element_type.65, (f32[4,4,128]{2,1,0:T(4,128)S(1)}, f32[4,4,128]{2,1,0:T(4,128)S(1)}, f32[4,4,128,128]{3,2,1,0:T(8,128)S(1)}) %tuple.50, (pred[128,1024]{0,1:T(8,128)(4,1)S(1)}, ...), branch_computations={%region_3.3_spmd, %region_4.6_spmd} | conditional | flops 1101533184 | bytes 38797348 | solution.py:127
  205.9 1.8 dynamic-slice_bitcast_fusion
  209.3 2.0 fusion.2
  211.4 3.1 %fusion.6 = f32[4,4,128,128]{3,2,1,0:T(8,128)S(1)} fusion(bf16[1024,4,128,1]{0,2,3,1:T(8,128)(2,1)S(1)} %bitcast.77, f32[4,1024,128,4]{2,1,3,0:T(8,128)S(1)} %get-tuple-element.167, f32[4,4,128]{2,1,0:T(4,128)S(1)} %max.3, pred[128,1024]{0,1:T(8,128)(4,1)S(1)} %get-tuple-element.79, f32[4,4,128,128]{3,2,1,0:T(8,128)S(1)} %get-tuple-element.84, ...), kind=kOutput, calls=%fused_computation.8 | convolution fusion | flops 547880960 | bytes 11681792 | tf_op jit(solution)/shard_map/while/body/eval_jaxpr/cond/branch_1_fun/gjtn,ngh->gjth/dot_general | solution.py:119
  216.0 8.6 %conditional.2 = ((f32[4,4,128]{2,1,0:T(4,128)S(1)}, f32[4,4,128]{2,1,0:T(4,128)S(1)}, f32[4,4,128,128]{3,2,1,0:T(8,128)S(1)})) conditional(s32[]{:T(128)} %convert_element_type.65, (f32[4,4,128]{2,1,0:T(4,128)S(1)}, f32[4,4,128]{2,1,0:T(4,128)S(1)}, f32[4,4,128,128]{3,2,1,0:T(8,128)S(1)}) %tuple.50, (pred[128,1024]{0,1:T(8,128)(4,1)S(1)}, ...), branch_computations={%region_3.3_spmd, %region_4.6_spmd} | conditional | flops 1101533184 | bytes 38797348 | solution.py:127
  216.0 1.8 dynamic-slice_bitcast_fusion
  219.5 2.0 fusion.2
  221.5 3.1 %fusion.6 = f32[4,4,128,128]{3,2,1,0:T(8,128)S(1)} fusion(bf16[1024,4,128,1]{0,2,3,1:T(8,128)(2,1)S(1)} %bitcast.77, f32[4,1024,128,4]{2,1,3,0:T(8,128)S(1)} %get-tuple-element.167, f32[4,4,128]{2,1,0:T(4,128)S(1)} %max.3, pred[128,1024]{0,1:T(8,128)(4,1)S(1)} %get-tuple-element.79, f32[4,4,128,128]{3,2,1,0:T(8,128)S(1)} %get-tuple-element.84, ...), kind=kOutput, calls=%fused_computation.8 | convolution fusion | flops 547880960 | bytes 11681792 | tf_op jit(solution)/shard_map/while/body/eval_jaxpr/cond/branch_1_fun/gjtn,ngh->gjth/dot_general | solution.py:119
  (70 shorter events, 19.8 us)
Async XLA Ops:
  0.0 1.2 copy-start
  1.2 10.8 %copy-start.2 = (s32[4,32]{1,0:T(4,128)S(1)}, s32[4,32]{1,0:T(4,128)}, u32[]{:S(2)}) copy-start(s32[4,32]{1,0:T(4,128)} %param.13) | copy-start | bytes 1540
  63.6 108.9 %all-to-all-start.1 = ((bf16[32,128,1024]{2,1,0:T(8,128)(2,1)}), bf16[32,128,1024]{2,1,0:T(8,128)(2,1)}, u32[]{:S(2)}, u32[]{:S(2)}) async-start(bf16[32,128,1024]{2,1,0:T(8,128)(2,1)} %stack.2), calls=%async_computation.1 | async-start | bytes 16777216 | tf_op jit(solution)/shard_map/all_to_all | solution.py:138
  224.7 2.0 copy-start.1
